TPU v7x, 32 devices: a whole 2x2x4 slice. The times are simulated.
32 devices in a mesh: gx: 4 (over x, core), gy: 4 (over z), zt: 2 (over y).
Axes of the slice: x: 2, y: 2, z: 4, core: 2. Of those that a mesh axis runs over, the one named last changes fastest.
Arguments:
- gauge_links: float32 [4, 2, 3, 3, 8, 32, 256], P(None, None, None, None, 'gx', 'gy', 'zt'), may hold values from -1 to 1, as said below
- momenta: float32 [4, 2, 3, 3, 8, 32, 256], P(None, None, None, None, 'gx', 'gy', 'zt'), may hold values from -4 to 4, as said below
Outputs:
- new_links: float32 [4, 2, 3, 3, 8, 32, 256], P(None, None, None, None, 'gx', 'gy', 'zt')
- new_momenta: float32 [4, 2, 3, 3, 8, 32, 256], P(None, None, None, None, 'gx', 'gy', 'zt')
- plaquette: float32 [], replicated
Inputs may be any that keep to these rules, and one draw needn't show every extreme that they name: `gauge_links`: every link is a unitary 3 x 3 complex matrix. `momenta`: every momentum is an antihermitian traceless 3 x 3 complex matrix.
All inputs are finite; a program needn't handle non-finite values.
Results may differ from a plain program's by a relative error of at most 0.0001.
Values sent between devices are 32-bit elements; how exact they have to be, the bound alone decides.
A program may use at most 128 MiB of HBM per device.

v0:
```python
import functools

import jax
import jax.numpy as jnp
from jax import lax
from jax.experimental import pallas as pl
from jax.experimental.pallas import tpu as pltpu
from jax.sharding import PartitionSpec as P

LT = 64
AXES = ("gx", "gy", "zt")
PAIRS = ((1, 3), (0, 3), (0, 1), (2, 3), (0, 2), (1, 2))
UPDATES = (3, 0, 2, 1)
MESH_ID = pl.DeviceIdType.MESH

kick_size = 0.25
step_size = 0.2


def mul(a, b):
    return a[0] * b[0] - a[1] * b[1], a[0] * b[1] + a[1] * b[0]


def mul_conj_second(a, b):
    return a[0] * b[0] + a[1] * b[1], a[1] * b[0] - a[0] * b[1]


def mul_conj_first(a, b):
    return a[0] * b[0] + a[1] * b[1], a[0] * b[1] - a[1] * b[0]


def add(a, b):
    return a[0] + b[0], a[1] + b[1]


def total(terms):
    result = terms[0]
    for term in terms[1:]:
        result = add(result, term)
    return result


def conj(a):
    return a[0], -a[1]


def pick(a, index):
    return a[0][index], a[1][index]


def kernel(
    sizes,
    volume,
    groups,
    links_in,
    mom_in,
    W,
    NM,
    plaq_out,
    V,
    MB,
    HB,
    TB,
    LB,
    YS,
    YR,
    ZS,
    ZR,
    YBS,
    YBR,
    ZBS,
    ZBR,
    TR,
    load_sem,
    fsend,
    frecv,
    bsend,
    brecv,
    tsend,
    trecv,
    *slots,
):
    coords = [lax.axis_index(axis) for axis in AXES]

    def device(offset):
        return tuple(
            lax.rem(coords[axis] + (offset[axis] % sizes[axis]), sizes[axis]) for axis in range(3)
        )

    def along(axis, distance):
        return tuple(distance if other == axis else 0 for other in range(3))

    loads = []
    for m in (3, 0, 1, 2):
        copy = pltpu.make_async_copy(links_in.at[m], V.at[m, :, :, :, 0:2], load_sem.at[m])
        copy.start()
        loads.append(copy)
    mom_load = pltpu.make_async_copy(mom_in, MB, load_sem.at[4])
    mom_load.start()

    barrier = pltpu.get_barrier_semaphore()
    partners = 0
    for axis in range(3):
        for k in range(1, sizes[axis]):
            pl.semaphore_signal(barrier, inc=1, device_id=device(along(axis, k)), device_id_type=MESH_ID)
            partners += 1

    shape3 = (1, 8, 128)
    lane = lax.broadcasted_iota(jnp.int32, shape3, 2)
    sub = lax.broadcasted_iota(jnp.int32, shape3, 1)
    t_index = lax.rem(lane, LT)
    half_lanes = lane.shape[-1] // 2
    low = lane < half_lanes
    t_last = t_index == LT - 1
    t_first = t_index == 0
    y_last = sub == 7
    y_first = sub == 0

    def choose(mask, a, b):
        return jnp.where(jnp.broadcast_to(mask, b.shape), jnp.broadcast_to(a, b.shape), b)

    pending = []

    def send(src, dst, offset, send_sem, recv_sem):
        copy = pltpu.make_async_remote_copy(
            src_ref=src,
            dst_ref=dst,
            send_sem=send_sem,
            recv_sem=recv_sem,
            device_id=device(offset),
            device_id_type=MESH_ID,
        )
        copy.start()
        pending.append(copy)
        return copy

    forward = {}
    backward = {}

    def send_link(stage, buf, m):
        for d in (2, 0, 1):
            if d == m:
                continue
            if d == 0:
                src, dst = buf.at[m, :, :, :, 0], buf.at[m, :, :, :, 2]
            elif d == 1:
                for r in range(2):
                    for i in range(3):
                        for x in range(2):
                            YS[stage, m, r, i, :, x] = buf[m, r, i, :, x, 0:1, :]
                src, dst = YS.at[stage, m], YR.at[stage, m]
            else:
                for r in range(2):
                    for i in range(3):
                        first = buf[m, r, i, :, 0]
                        second = buf[m, r, i, :, 1]
                        ZS[stage, m, r, i] = choose(low, first, pltpu.roll(second, half_lanes, 2))
                src, dst = ZS.at[stage, m], ZR.at[stage, m]
            forward[stage, d, m] = send(
                src, dst, along(d, -1), fsend.at[stage, d, m], frecv.at[stage, d, m]
            )

    def send_back(stage, d, m):
        if d == 3:
            return
        if d == 0:
            src, dst = LB.at[stage, 0, m, :, 2], LB.at[stage, 0, m, :, 0]
        elif d == 1:
            for x in range(2):
                YBS[stage, m, :, x] = LB[stage, 1, m, :, x + 1, 7:8, :]
            src, dst = YBS.at[stage, m], YBR.at[stage, m]
        else:
            first = LB[stage, 2, m, :, 1]
            second = LB[stage, 2, m, :, 2]
            ZBS[stage, m] = choose(low, pltpu.roll(first, half_lanes, 2), second)
            src, dst = ZBS.at[stage, m], ZBR.at[stage, m]
        backward[stage, d, m] = send(src, dst, along(d, 1), bsend.at[stage, d, m], brecv.at[stage, d, m])

    def ahead(stage, buf, n, d, x):
        rows = []
        for k in range(3):
            parts = []
            for r in range(2):
                if d == 0:
                    parts.append(buf[n, r, k, :, x + 1])
                    continue
                value = buf[n, r, k, :, x]
                if d == 3:
                    parts.append(
                        choose(t_last, pltpu.roll(value, LT - 1, 2), pltpu.roll(value, 127, 2))
                    )
                elif d == 1:
                    parts.append(choose(y_last, YR[stage, n, r, k, :, x], pltpu.roll(value, 7, 1)))
                else:
                    halo = pltpu.roll(ZR[stage, n, r, k], half_lanes * (1 - x), 2)
                    parts.append(choose(low, pltpu.roll(value, half_lanes, 2), halo))
            rows.append(tuple(parts))
        return rows

    def behind(stage, d, m, x):
        if d == 0:
            return LB[stage, 0, m, :, x]
        value = LB[stage, d, m, :, x + 1]
        if d == 1:
            return choose(y_first, YBR[stage, m, :, x], pltpu.roll(value, 1, 1))
        if d == 2:
            halo = pltpu.roll(ZBR[stage, m], half_lanes * x, 2)
            return choose(low, halo, pltpu.roll(value, half_lanes, 2))
        return choose(t_first, pltpu.roll(value, 128 - (LT - 1), 2), pltpu.roll(value, 1, 2))

    def conjugate(T, rows):
        d0, d1, d2, h01, h02, h12 = T
        full = [
            [d0, h01, h02],
            [(-h01[0], h01[1]), d1, h12],
            [(-h02[0], h02[1]), (-h12[0], h12[1]), d2],
        ]
        M = []
        for i in range(3):
            terms = []
            for k in range(3):
                if i == k:
                    terms.append((-(full[i][i] * rows[k][1]), full[i][i] * rows[k][0]))
                else:
                    terms.append(mul(full[i][k], rows[k]))
            M.append(total(terms))
        r0 = 0.0
        r1 = 0.0
        for k in range(3):
            r0 = r0 + (rows[k][0][0] * M[k][1][0] - rows[k][1][0] * M[k][0][0])
            r1 = r1 + (rows[k][0][1] * M[k][1][1] - rows[k][1][1] * M[k][0][1])
        tail = slice(1, 3)
        row0 = total(
            [mul_conj_first(pick(rows[k], 0), (M[k][0][tail], M[k][1][tail])) for k in range(3)]
        )
        r12 = total([mul_conj_first(pick(rows[k], 1), pick(M[k], 2)) for k in range(3)])
        return [r0, r1, row0[0][0], row0[1][0], row0[0][1], row0[1][1], r12[0], r12[1]]

    def pair_task(stage, buf, m, n, x):
        index = PAIRS.index((m, n))
        n_ahead = ahead(stage, buf, n, m, x)
        A = []
        for i in range(3):
            A.append(
                total(
                    [mul((buf[m, 0, i, k, x], buf[m, 1, i, k, x]), n_ahead[k]) for k in range(3)]
                )
            )
        m_ahead = ahead(stage, buf, m, n, x)
        columns = [(buf[n, 0, :, l, x], buf[n, 1, :, l, x]) for l in range(3)]
        Bt = []
        for k in range(3):
            Bt.append(total([mul(pick(m_ahead[l], k), columns[l]) for l in range(3)]))
        loop = []
        for i in range(3):
            loop.append(total([mul_conj_second(pick(A[i], k), Bt[k]) for k in range(3)]))
        i0, i1, i2 = loop[0][1][0], loop[1][1][1], loop[2][1][2]
        mean = (i0 + i1 + i2) * (2.0 / 3.0)
        d0 = 2.0 * i0 - mean
        d1 = 2.0 * i1 - mean
        d2 = -(d0 + d1)

        def off(i, j):
            a = pick(loop[i], j)
            b = pick(loop[j], i)
            return a[0] - b[0], a[1] + b[1]

        h01, h02, h12 = off(0, 1), off(0, 2), off(1, 2)
        values = [d0, d1, h01[0], h01[1], h02[0], h02[1], h12[0], h12[1]]
        for c in range(8):
            TB[index, c, x] = values[c]
        if stage == 1:
            trace = loop[0][0][0] + loop[1][0][1] + loop[2][0][2]
            TR[x] = trace if index == 0 else TR[x] + trace
        T = (d0, d1, d2, h01, h02, h12)
        for link, d in ((m, n), (n, m)):
            rows = [(buf[d, 0, k, :, x], buf[d, 1, k, :, x]) for k in range(3)]
            result = conjugate(T, rows)
            for c in range(8):
                LB[stage, d, link, c, x + 1] = result[c]

    def force(stage, m, x):
        result = None
        for n in range(4):
            if n == m:
                continue
            index = PAIRS.index((min(m, n), max(m, n)))
            term = TB[index, :, x] - behind(stage, n, m, x)
            if result is None:
                result = term if m < n else -term
            else:
                result = result + term if m < n else result - term
        return result

    places = ((1, 0, 0), (1, 1, 1), (0, 0, 1), (1, 0, 1), (0, 0, 2), (1, 0, 2), (0, 1, 2), (1, 1, 2))

    def first_update(m, x):
        F = force(0, m, x)
        half = []
        for c, (r, i, j) in enumerate(places):
            value = MB[m, r, i, j, x] - (0.5 * kick_size) * F[c]
            HB[m, c, x] = value
            half.append((0.5 * step_size) * value)
        d0, d1 = half[0], half[1]
        d2 = -(d0 + d1)
        h01, h02, h12 = (half[2], half[3]), (half[4], half[5]), (half[6], half[7])
        n01 = h01[0] * h01[0] + h01[1] * h01[1]
        n02 = h02[0] * h02[0] + h02[1] * h02[1]
        n12 = h12[0] * h12[0] + h12[1] * h12[1]
        k00 = d0 * d0 + n01 + n02
        k11 = d1 * d1 + n01 + n12
        k22 = d2 * d2 + n02 + n12
        one_c = 1.0 + 0.5 * (k00 + k11 + k22)
        h01h12 = mul(h01, h12)
        z_imag = h01h12[1] * h02[0] - h01h12[0] * h02[1]
        h = d0 * n12 + d2 * n01 + d1 * n02 - d0 * d1 * d2 - 2.0 * z_imag
        factor = 2.0 / (one_c * one_c + h * h)
        f = (one_c * factor, h * factor)
        s01 = mul_conj_second(h02, h12)
        k01 = (-(d0 + d1) * h01[1] - s01[0], (d0 + d1) * h01[0] - s01[1])
        k02 = (h01h12[0] - (d0 + d2) * h02[1], h01h12[1] + (d0 + d2) * h02[0])
        s12 = mul_conj_first(h01, h02)
        k12 = (-s12[0] - (d1 + d2) * h12[1], (d1 + d2) * h12[0] - s12[1])
        G = [[None] * 3 for _ in range(3)]
        for i, (k, d) in enumerate(((k00, d0), (k11, d1), (k22, d2))):
            G[i][i] = (one_c - k, d)
        for i, j, hh, kk in ((0, 1, h01, k01), (0, 2, h02, k02), (1, 2, h12, k12)):
            G[i][j] = add(hh, kk)
            G[j][i] = (kk[0] - hh[0], hh[1] - kk[1])
        rows = [(V[m, 0, k, :, x], V[m, 1, k, :, x]) for k in range(3)]
        for i in range(3):
            E = []
            for k in range(3):
                value = mul(f, G[i][k])
                E.append((value[0] - 1.0, value[1]) if i == k else value)
            new = total([mul(E[k], rows[k]) for k in range(3)])
            W[m, 0, i, :, x] = new[0]
            W[m, 1, i, :, x] = new[1]

    def last_update(m, x):
        F = force(1, m, x)
        v = [HB[m, c, x] - (0.5 * kick_size) * F[c] for c in range(8)]
        zero = jnp.zeros_like(v[0])
        for i in range(3):
            NM[m, 0, i, i, x] = zero
        NM[m, 1, 0, 0, x] = v[0]
        NM[m, 1, 1, 1, x] = v[1]
        NM[m, 1, 2, 2, x] = -(v[0] + v[1])
        for i, j, c in ((0, 1, 2), (0, 2, 4), (1, 2, 6)):
            NM[m, 0, i, j, x] = v[c]
            NM[m, 0, j, i, x] = -v[c]
            NM[m, 1, i, j, x] = v[c + 1]
            NM[m, 1, j, i, x] = v[c + 1]

    def for_x(body):
        def step(x, carry):
            body(x)
            return carry

        lax.fori_loop(0, 2, step, 0)

    def pairs_of(stage, buf):
        for m, n in PAIRS:
            for link, d in ((n, m), (m, n)):
                if d != 3:
                    forward[stage, d, link].wait_recv()
            for_x(lambda x: pair_task(stage, buf, m, n, x))
            for link, d in ((m, n), (n, m)):
                send_back(stage, d, link)

    def wait_back(stage, m):
        for d in range(3):
            if d != m:
                backward[stage, d, m].wait_recv()

    for position, m in enumerate((3, 0, 1, 2)):
        loads[position].wait()
        if position == 0:
            pl.semaphore_wait(barrier, partners)
        send_link(0, V, m)
    pairs_of(0, V)
    mom_load.wait()
    for m in UPDATES:
        wait_back(0, m)
        for_x(lambda x: first_update(m, x))
        send_link(1, W, m)
    pairs_of(1, W)

    def offsets(group):
        result = [()]
        for axis in range(3):
            span = range(sizes[axis]) if axis in group else (0,)
            result = [head + (k,) for head in result for k in span]
        return [item for item in result if any(item)]

    def spread(index, value):
        buf = slots[index]
        position = 0
        for axis in groups[index]:
            position = position * sizes[axis] + coords[axis]
        buf[position] = jnp.sum(value, axis=0, keepdims=True)
        copies = []
        for k, offset in enumerate(offsets(groups[index])):
            copies.append(
                send(
                    buf.at[position],
                    buf.at[position],
                    offset,
                    tsend.at[index, k],
                    trecv.at[index, k],
                )
            )
        return copies

    def gathered(index, copies):
        for copy in copies:
            copy.wait_recv()
        value = slots[index][0]
        for k in range(1, slots[index].shape[0]):
            value = value + slots[index][k]
        return value

    def finish(m):
        wait_back(1, m)
        for_x(lambda x: last_update(m, x))

    value = TR[0] + TR[1]
    copies = spread(0, value)
    for position, m in enumerate(UPDATES):
        finish(m)
        if position + 1 < len(groups):
            value = gathered(position, copies)
            copies = spread(position + 1, value)
    plaq_out[0] = jnp.sum(gathered(len(groups) - 1, copies)) * (4.0 / (72.0 * volume))
    for copy in pending:
        copy.wait_send()


def store_kernel(links, mom, links_out, mom_out, sem):
    copies = []
    for m in range(4):
        copies.append(
            pltpu.make_async_copy(links.at[m, :, :, :, 0:2], links_out.at[m], sem.at[m])
        )
        copies.append(pltpu.make_async_copy(mom.at[m], mom_out.at[m], sem.at[4 + m]))
    for copy in copies:
        copy.start()
    for copy in copies:
        copy.wait()


def per_device(gauge_links, momenta):
    block = gauge_links.shape
    assert block[-3:] == (2, 8, 2 * LT)
    sizes = tuple(lax.axis_size(axis) for axis in AXES)
    sites = block[-3] * block[-2] * block[-1]
    volume = sites * sizes[0] * sizes[1] * sizes[2]
    f32 = jnp.float32
    vm = lambda *shape: pltpu.VMEM(shape, f32)
    groups = ((0, 1, 2),) if sizes[0] * sizes[1] * sizes[2] <= 32 else ((0,), (1,), (2,))
    counts = []
    for group in groups:
        count = 1
        for axis in group:
            count *= sizes[axis]
        counts.append(count)
    dma = pltpu.SemaphoreType.DMA
    wide_links, momenta_vmem, plaquette = pl.pallas_call(
        functools.partial(kernel, sizes, volume, groups),
        out_shape=(
            vm(4, 2, 3, 3, 3, 8, 128),
            vm(*block),
            jax.ShapeDtypeStruct((1,), f32),
        ),
        in_specs=[pl.BlockSpec(memory_space=pl.ANY)] * 2,
        out_specs=(
            pl.BlockSpec(memory_space=pltpu.VMEM),
            pl.BlockSpec(memory_space=pltpu.VMEM),
            pl.BlockSpec(memory_space=pltpu.SMEM),
        ),
        scratch_shapes=[
            vm(4, 2, 3, 3, 3, 8, 128),
            vm(*block),
            vm(4, 8, 2, 8, 128),
            vm(6, 8, 2, 8, 128),
            vm(2, 4, 4, 8, 3, 8, 128),
            vm(2, 4, 2, 3, 3, 2, 1, 128),
            vm(2, 4, 2, 3, 3, 2, 1, 128),
            vm(2, 4, 2, 3, 3, 8, 128),
            vm(2, 4, 2, 3, 3, 8, 128),
            vm(2, 4, 8, 2, 1, 128),
            vm(2, 4, 8, 2, 1, 128),
            vm(2, 4, 8, 8, 128),
            vm(2, 4, 8, 8, 128),
            vm(2, 8, 128),
            dma((5,)),
            dma((2, 3, 4)),
            dma((2, 3, 4)),
            dma((2, 3, 4)),
            dma((2, 3, 4)),
            dma((len(groups), max(counts))),
            dma((len(groups), max(counts))),
            *[vm(count, 1, 128) for count in counts],
        ],
        compiler_params=pltpu.CompilerParams(collective_id=0, has_side_effects=True),
        name="md_step",
    )(gauge_links, momenta)
    anywhere = pl.BlockSpec(memory_space=pl.ANY)
    in_vmem = pl.BlockSpec(memory_space=pltpu.VMEM)
    new_links, new_momenta = pl.pallas_call(
        store_kernel,
        out_shape=(jax.ShapeDtypeStruct(block, f32),) * 2,
        in_specs=[in_vmem, in_vmem],
        out_specs=(anywhere, anywhere),
        scratch_shapes=[dma((8,))],
        name="store",
    )(
        pltpu.with_memory_space_constraint(wide_links, pltpu.VMEM),
        pltpu.with_memory_space_constraint(momenta_vmem, pltpu.VMEM),
    )
    return new_links, new_momenta, plaquette.reshape(())


def solution(mesh):
    spec = P(None, None, None, None, "gx", "gy", "zt")
    return jax.shard_map(
        per_device,
        mesh=mesh,
        in_specs=(spec, spec),
        out_specs=(spec, spec, P()),
        check_vma=False,
    )
```

profile of v0, /device:TPU:0, one launch (start us, length us, event | category | flops | bytes accessed | tf_op | source)
XLA Modules:
  0.0 31.4 jit_solution(5694433001541981132)
XLA Ops:
  0.6 27.9 %md_step.1 = (f32[4,2,3,3,3,8,128]{6,5,4,3,2,1,0:T(8,128)S(1)}, f32[4,2,3,3,2,8,128]{6,5,4,3,2,1,0:T(8,128)S(1)}, f32[1]{0:T(128)}) custom-call(f32[4,2,3,3,2,8,128]{6,5,4,3,2,1,0:T(8,128)} %links_in.1, f32[4,2,3,3,2,8,128]{6,5,4,3,2,1,0:T(8,128)} %mom_in.1), custom_call_target="tpu_custom_call" | custom-call | tf_op jit(solution)/shard_map/md_step/pallas_call | solution.py:468
  28.5 1.1 %store.1 = (f32[4,2,3,3,2,8,128]{6,5,4,3,2,1,0:T(8,128)}, f32[4,2,3,3,2,8,128]{6,5,4,3,2,1,0:T(8,128)}) custom-call(f32[4,2,3,3,3,8,128]{6,5,4,3,2,1,0:T(8,128)S(1)} %get-tuple-element.8.links, f32[4,2,3,3,2,8,128]{6,5,4,3,2,1,0:T(8,128)S(1)} %get-tuple-element.9.mom), custom_call_target="tpu_custom_call" | custom-call | tf_op jit(solution)/shard_map/store/pallas_call | solution.py:510
where the time goes:
time: 31.5 us; the launch traced here: 31.4 us
  Pallas kernels  29 us (92%)
  between operations  2.4 us (8%)
    pallas_call x1, Pallas kernels, per_device(): pl.pallas_call(functools.partial(kernel, sizes, volume, groups), out_shap...  27.9 us
    pallas_call x1, Pallas kernels, per_device(): pl.pallas_call(store_kernel, out_shape=(jax.ShapeDtypeStruct(block, f32),...  1.07 us

commit v1 on v0

--- a/solution.py
+++ b/solution.py
@@ -46,6 +46,62 @@
 
 def pick(a, index):
     return a[0][index], a[1][index]
+
+
+TINY = 1e-30
+FAR = 1e15
+CODED = 11
+
+
+def project(first, rest):
+    square = rest[0] * rest[0]
+    for value in rest[1:]:
+        square = square + value * value
+    near = first >= 0.0
+    low = jnp.where(near, 1.0 + first, square)
+    factor = jnp.where(near, 1.0, 1.0 - first) / jnp.maximum(low, TINY)
+    result = [value * factor for value in rest]
+    result[0] = jnp.where(low < TINY, FAR, result[0])
+    return result
+
+
+def lift(values):
+    square = values[0] * values[0]
+    for value in values[1:]:
+        square = square + value * value
+    inverse = 1.0 / (1.0 + square)
+    double = 2.0 * inverse
+    return [(1.0 - square) * inverse] + [value * double for value in values]
+
+
+def cross(a, b):
+    result = []
+    for i in range(3):
+        j, k = (i + 1) % 3, (i + 2) % 3
+        p, q = mul(a[j], b[k]), mul(a[k], b[j])
+        result.append((p[0] - q[0], p[1] - q[1]))
+    return result
+
+
+def encode(rows):
+    rows = [[pick(row, l) for l in range(3)] for row in rows]
+    normal = cross(rows[0], rows[1])
+    det = total([mul(rows[2][l], normal[l]) for l in range(3)])
+    values = []
+    for row in rows[:2]:
+        flat = [part for entry in row for part in entry]
+        values += project(flat[0], flat[1:])
+    return values + project(det[0], [det[1]])
+
+
+def decode(values):
+    rows = []
+    for start in (0, 5):
+        flat = lift(values[start : start + 5])
+        rows.append([(flat[2 * l], flat[2 * l + 1]) for l in range(3)])
+    det = lift(values[10:])
+    rows.append([mul_conj_second(det, entry) for entry in cross(rows[0], rows[1])])
+    return rows
 
 
 def kernel(
@@ -64,8 +120,13 @@
     LB,
     YS,
     YR,
+    YHS,
+    YHR,
     ZS,
     ZR,
+    ZHS,
+    ZHR,
+    ZL,
     YBS,
     YBR,
     ZBS,
@@ -137,28 +198,53 @@
     forward = {}
     backward = {}
 
-    def send_link(stage, buf, m):
+    def forward_send(stage, d, m, src, dst):
+        forward[stage, d, m] = send(
+            src, dst, along(d, -1), fsend.at[stage, d, m], frecv.at[stage, d, m]
+        )
+
+    def send_link(m):
         for d in (2, 0, 1):
             if d == m:
                 continue
             if d == 0:
-                src, dst = buf.at[m, :, :, :, 0], buf.at[m, :, :, :, 2]
+                src, dst = V.at[m, :, :, :, 0], V.at[m, :, :, :, 2]
             elif d == 1:
                 for r in range(2):
                     for i in range(3):
                         for x in range(2):
-                            YS[stage, m, r, i, :, x] = buf[m, r, i, :, x, 0:1, :]
-                src, dst = YS.at[stage, m], YR.at[stage, m]
+                            YS[m, r, i, :, x : x + 1] = V[m, r, i, :, x, 0:1, :]
+                src, dst = YS.at[m], YR.at[0, m]
             else:
-                for r in range(2):
-                    for i in range(3):
-                        first = buf[m, r, i, :, 0]
-                        second = buf[m, r, i, :, 1]
-                        ZS[stage, m, r, i] = choose(low, first, pltpu.roll(second, half_lanes, 2))
-                src, dst = ZS.at[stage, m], ZR.at[stage, m]
-            forward[stage, d, m] = send(
-                src, dst, along(d, -1), fsend.at[stage, d, m], frecv.at[stage, d, m]
-            )
+                rows = []
+                for i in range(3):
+                    parts = []
+                    for r in range(2):
+                        first = V[m, r, i, :, 0]
+                        second = V[m, r, i, :, 1]
+                        parts.append(choose(low, first, pltpu.roll(second, half_lanes, 2)))
+                    rows.append(tuple(parts))
+                for c, value in enumerate(encode(rows)):
+                    ZS[m, c] = value
+                src, dst = ZS.at[m], ZR.at[m]
+            forward_send(0, d, m, src, dst)
+
+    def send_half(m):
+        for d in (2, 0, 1):
+            if d == m:
+                continue
+            if d == 0:
+                src, dst = HB.at[m, :, 0], HB.at[m, :, 2]
+            elif d == 1:
+                for x in range(2):
+                    YHS[m, :, x : x + 1] = HB[m, :, x, 0:1, :]
+                src, dst = YHS.at[m], YHR.at[m]
+            else:
+                first = HB[m, :, 0]
+                second = HB[m, :, 1]
+                ZHS[m] = choose(low, first, pltpu.roll(second, half_lanes, 2))
+                src, dst = ZHS.at[m], ZHR.at[m]
+            forward_send(1, d, m, src, dst)
 
     def send_back(stage, d, m):
         if d == 3:
@@ -190,9 +276,10 @@
                         choose(t_last, pltpu.roll(value, LT - 1, 2), pltpu.roll(value, 127, 2))
                     )
                 elif d == 1:
-                    parts.append(choose(y_last, YR[stage, n, r, k, :, x], pltpu.roll(value, 7, 1)))
+                    row = YR[stage, n, r, k, :, pl.ds(x, 1)]
+                    parts.append(choose(y_last, row, pltpu.roll(value, 7, 1)))
                 else:
-                    halo = pltpu.roll(ZR[stage, n, r, k], half_lanes * (1 - x), 2)
+                    halo = pltpu.roll(ZL[stage, n, r, k], half_lanes * (1 - x), 2)
                     parts.append(choose(low, pltpu.roll(value, half_lanes, 2), halo))
             rows.append(tuple(parts))
         return rows
@@ -294,13 +381,13 @@
 
     places = ((1, 0, 0), (1, 1, 1), (0, 0, 1), (1, 0, 1), (0, 0, 2), (1, 0, 2), (0, 1, 2), (1, 1, 2))
 
-    def first_update(m, x):
+    def half_update(m, x):
         F = force(0, m, x)
-        half = []
         for c, (r, i, j) in enumerate(places):
-            value = MB[m, r, i, j, x] - (0.5 * kick_size) * F[c]
-            HB[m, c, x] = value
-            half.append((0.5 * step_size) * value)
+            HB[m, c, x] = MB[m, r, i, j, x] - (0.5 * kick_size) * F[c]
+
+    def cayley(momentum, rows):
+        half = [(0.5 * step_size) * value for value in momentum]
         d0, d1 = half[0], half[1]
         d2 = -(d0 + d1)
         h01, h02, h12 = (half[2], half[3]), (half[4], half[5]), (half[6], half[7])
@@ -327,15 +414,39 @@
         for i, j, hh, kk in ((0, 1, h01, k01), (0, 2, h02, k02), (1, 2, h12, k12)):
             G[i][j] = add(hh, kk)
             G[j][i] = (kk[0] - hh[0], hh[1] - kk[1])
-        rows = [(V[m, 0, k, :, x], V[m, 1, k, :, x]) for k in range(3)]
+        result = []
         for i in range(3):
             E = []
             for k in range(3):
                 value = mul(f, G[i][k])
                 E.append((value[0] - 1.0, value[1]) if i == k else value)
-            new = total([mul(E[k], rows[k]) for k in range(3)])
-            W[m, 0, i, :, x] = new[0]
-            W[m, 1, i, :, x] = new[1]
+            result.append(total([mul(E[k], rows[k]) for k in range(3)]))
+        return result
+
+    def link_update(m, x):
+        rows = [(V[m, 0, k, :, x], V[m, 1, k, :, x]) for k in range(3)]
+        new = cayley([HB[m, c, x] for c in range(8)], rows)
+        for i in range(3):
+            W[m, 0, i, :, x] = new[i][0]
+            W[m, 1, i, :, x] = new[i][1]
+
+    def halo_update(d, m):
+        if d == 0:
+            link_update(m, 2)
+            return
+        buf, momentum = (YR, YHR) if d == 1 else (ZL, ZHR)
+        rows = [(buf[0, m, 0, k], buf[0, m, 1, k]) for k in range(3)]
+        new = cayley([momentum[m, c] for c in range(8)], rows)
+        for i in range(3):
+            buf[1, m, 0, i] = new[i][0]
+            buf[1, m, 1, i] = new[i][1]
+
+    def halo_decode(m):
+        rows = decode([ZR[m, c] for c in range(CODED)])
+        for k in range(3):
+            for r in range(2):
+                for l in range(3):
+                    ZL[0, m, r, k, l] = rows[k][l][r]
 
     def last_update(m, x):
         F = force(1, m, x)
@@ -362,8 +473,14 @@
     def pairs_of(stage, buf):
         for m, n in PAIRS:
             for link, d in ((n, m), (m, n)):
-                if d != 3:
+                if d == 3:
+                    continue
+                with jax.named_scope(f"wf{stage}_d{d}m{link}"):
                     forward[stage, d, link].wait_recv()
+                if stage == 1:
+                    halo_update(d, link)
+                elif d == 2:
+                    halo_decode(link)
             for_x(lambda x: pair_task(stage, buf, m, n, x))
             for link, d in ((m, n), (n, m)):
                 send_back(stage, d, link)
@@ -376,14 +493,17 @@
     for position, m in enumerate((3, 0, 1, 2)):
         loads[position].wait()
         if position == 0:
-            pl.semaphore_wait(barrier, partners)
-        send_link(0, V, m)
+            with jax.named_scope("bar"):
+                pl.semaphore_wait(barrier, partners)
+        send_link(m)
     pairs_of(0, V)
     mom_load.wait()
     for m in UPDATES:
-        wait_back(0, m)
-        for_x(lambda x: first_update(m, x))
-        send_link(1, W, m)
+        with jax.named_scope(f"wb0_{m}"):
+            wait_back(0, m)
+        for_x(lambda x: half_update(m, x))
+        send_half(m)
+        for_x(lambda x: link_update(m, x))
     pairs_of(1, W)
 
     def offsets(group):
@@ -421,7 +541,8 @@
         return value
 
     def finish(m):
-        wait_back(1, m)
+        with jax.named_scope(f"wb1_{m}"):
+            wait_back(1, m)
         for_x(lambda x: last_update(m, x))
 
     value = TR[0] + TR[1]
@@ -431,13 +552,15 @@
         if position + 1 < len(groups):
             value = gathered(position, copies)
             copies = spread(position + 1, value)
-    plaq_out[0] = jnp.sum(gathered(len(groups) - 1, copies)) * (4.0 / (72.0 * volume))
+    with jax.named_scope("plaq"):
+        lanes = gathered(len(groups) - 1, copies) * (4.0 / (72.0 * volume))
+        plaq_out[...] = jnp.sum(lanes, axis=1, keepdims=True)
     for copy in pending:
         copy.wait_send()
 
 
-def store_kernel(links, mom, links_out, mom_out, sem):
-    copies = []
+def store_kernel(links, mom, plaq, links_out, mom_out, plaq_out, sem):
+    copies = [pltpu.make_async_copy(plaq, plaq_out, sem.at[8])]
     for m in range(4):
         copies.append(
             pltpu.make_async_copy(links.at[m, :, :, :, 0:2], links_out.at[m], sem.at[m])
@@ -470,23 +593,28 @@
         out_shape=(
             vm(4, 2, 3, 3, 3, 8, 128),
             vm(*block),
-            jax.ShapeDtypeStruct((1,), f32),
+            vm(1, 1),
         ),
         in_specs=[pl.BlockSpec(memory_space=pl.ANY)] * 2,
         out_specs=(
             pl.BlockSpec(memory_space=pltpu.VMEM),
             pl.BlockSpec(memory_space=pltpu.VMEM),
-            pl.BlockSpec(memory_space=pltpu.SMEM),
+            pl.BlockSpec(memory_space=pltpu.VMEM),
         ),
         scratch_shapes=[
             vm(4, 2, 3, 3, 3, 8, 128),
             vm(*block),
-            vm(4, 8, 2, 8, 128),
+            vm(4, 8, 3, 8, 128),
             vm(6, 8, 2, 8, 128),
             vm(2, 4, 4, 8, 3, 8, 128),
-            vm(2, 4, 2, 3, 3, 2, 1, 128),
-            vm(2, 4, 2, 3, 3, 2, 1, 128),
-            vm(2, 4, 2, 3, 3, 8, 128),
+            vm(4, 2, 3, 3, 2, 128),
+            vm(2, 4, 2, 3, 3, 2, 128),
+            vm(4, 8, 2, 128),
+            vm(4, 8, 2, 128),
+            vm(4, CODED, 8, 128),
+            vm(4, CODED, 8, 128),
+            vm(4, 8, 8, 128),
+            vm(4, 8, 8, 128),
             vm(2, 4, 2, 3, 3, 8, 128),
             vm(2, 4, 8, 2, 1, 128),
             vm(2, 4, 8, 2, 1, 128),
@@ -507,16 +635,21 @@
     )(gauge_links, momenta)
     anywhere = pl.BlockSpec(memory_space=pl.ANY)
     in_vmem = pl.BlockSpec(memory_space=pltpu.VMEM)
-    new_links, new_momenta = pl.pallas_call(
+    new_links, new_momenta, plaquette = pl.pallas_call(
         store_kernel,
-        out_shape=(jax.ShapeDtypeStruct(block, f32),) * 2,
-        in_specs=[in_vmem, in_vmem],
-        out_specs=(anywhere, anywhere),
-        scratch_shapes=[dma((8,))],
+        out_shape=(
+            jax.ShapeDtypeStruct(block, f32),
+            jax.ShapeDtypeStruct(block, f32),
+            jax.ShapeDtypeStruct((1, 1), f32),
+        ),
+        in_specs=[in_vmem] * 3,
+        out_specs=(anywhere,) * 3,
+        scratch_shapes=[dma((9,))],
         name="store",
     )(
         pltpu.with_memory_space_constraint(wide_links, pltpu.VMEM),
         pltpu.with_memory_space_constraint(momenta_vmem, pltpu.VMEM),
+        pltpu.with_memory_space_constraint(plaquette, pltpu.VMEM),
     )
     return new_links, new_momenta, plaquette.reshape(())
 

time: 31.5 us -> 30.3 us (0.962)
  between operations: 2.4 us -> 0.64 us
  Pallas kernels: 29 us -> 29.5 us
    pallas_call x1, Pallas kernels: 1.07 us -> 1.72 us  [per_device(): pl.pallas_call(store_kernel, out_shape=(jax.ShapeDtypeStruct(block, f32),...]
where the time goes in v1:
time: 30.3 us; the launch traced here: 30.2 us
  Pallas kernels  29.5 us (97%)
  between operations  0.64 us (2%)
    pallas_call x1, Pallas kernels, per_device(): pl.pallas_call(functools.partial(kernel, sizes, volume, groups), out_shap...  27.8 us
    pallas_call x1, Pallas kernels, per_device(): pl.pallas_call(store_kernel, out_shape=(jax.ShapeDtypeStruct(block, f32),...  1.72 us

profile of v1, /device:TPU:0, one launch (start us, length us, event | category | flops | bytes accessed | tf_op | source)
XLA Modules:
  0.0 30.2 jit_solution(10568834385698246847)
XLA Ops:
  0.6 27.8 %md_step.1 = (f32[4,2,3,3,3,8,128]{6,5,4,3,2,1,0:T(8,128)S(1)}, f32[4,2,3,3,2,8,128]{6,5,4,3,2,1,0:T(8,128)S(1)}, f32[1,1]{1,0:T(1,128)}) custom-call(f32[4,2,3,3,2,8,128]{6,5,4,3,2,1,0:T(8,128)} %links_in.1, f32[4,2,3,3,2,8,128]{6,5,4,3,2,1,0:T(8,128)} %mom_in.1), custom_call_target="tpu_custom_call" | custom-call | tf_op jit(solution)/shard_map/md_step/pallas_call | solution.py:591
  28.4 1.7 %store.1 = (f32[4,2,3,3,2,8,128]{6,5,4,3,2,1,0:T(8,128)}, f32[4,2,3,3,2,8,128]{6,5,4,3,2,1,0:T(8,128)}, f32[1,1]{1,0:T(1,128)}) custom-call(f32[4,2,3,3,3,8,128]{6,5,4,3,2,1,0:T(8,128)S(1)} %get-tuple-element.9.links, f32[4,2,3,3,2,8,128]{6,5,4,3,2,1,0:T(8,128)S(1)} %get-tuple-element.10.mom, f32[1,1]{1,0:T(1,128)} %get-tuple-element.11.plaq), custom_call_target="tpu_custom_call" | custom-call | tf_op jit(solution)/shard_map/store/pallas_call | solution.py:638

commit v2 on v1

--- a/solution.py
+++ b/solution.py
@@ -554,13 +554,13 @@
             copies = spread(position + 1, value)
     with jax.named_scope("plaq"):
         lanes = gathered(len(groups) - 1, copies) * (4.0 / (72.0 * volume))
-        plaq_out[...] = jnp.sum(lanes, axis=1, keepdims=True)
+        plaq_out[...] = jnp.broadcast_to(jnp.sum(lanes, axis=1, keepdims=True), (8, 128))
     for copy in pending:
         copy.wait_send()
 
 
 def store_kernel(links, mom, plaq, links_out, mom_out, plaq_out, sem):
-    copies = [pltpu.make_async_copy(plaq, plaq_out, sem.at[8])]
+    copies = [pltpu.make_async_copy(plaq.at[0:1], plaq_out, sem.at[8])]
     for m in range(4):
         copies.append(
             pltpu.make_async_copy(links.at[m, :, :, :, 0:2], links_out.at[m], sem.at[m])
@@ -593,7 +593,7 @@
         out_shape=(
             vm(4, 2, 3, 3, 3, 8, 128),
             vm(*block),
-            vm(1, 1),
+            vm(8, 128),
         ),
         in_specs=[pl.BlockSpec(memory_space=pl.ANY)] * 2,
         out_specs=(
@@ -640,7 +640,7 @@
         out_shape=(
             jax.ShapeDtypeStruct(block, f32),
             jax.ShapeDtypeStruct(block, f32),
-            jax.ShapeDtypeStruct((1, 1), f32),
+            jax.ShapeDtypeStruct((1, 128), f32),
         ),
         in_specs=[in_vmem] * 3,
         out_specs=(anywhere,) * 3,
@@ -651,7 +651,7 @@
         pltpu.with_memory_space_constraint(momenta_vmem, pltpu.VMEM),
         pltpu.with_memory_space_constraint(plaquette, pltpu.VMEM),
     )
-    return new_links, new_momenta, plaquette.reshape(())
+    return new_links, new_momenta, plaquette[0, 0]
 
 
 def solution(mesh):

time: 30.3 us -> 29.1 us (0.960)
  Pallas kernels: 29.5 us -> 28.4 us
    pallas_call x1, Pallas kernels: 1.72 us -> 1.09 us  [per_device(): pl.pallas_call(store_kernel, out_shape=(jax.ShapeDtypeStruct(block, f32),...]
    pallas_call x1, Pallas kernels: 27.8 us -> 27.3 us  [per_device(): pl.pallas_call(functools.partial(kernel, sizes, volume, groups), out_shap...]
where the time goes in v2:
time: 29.1 us; the launch traced here: 29 us
  Pallas kernels  28.4 us (98%)
  between operations  0.64 us (2%)
    pallas_call x1, Pallas kernels, per_device(): pl.pallas_call(functools.partial(kernel, sizes, volume, groups), out_shap...  27.3 us
    pallas_call x1, Pallas kernels, per_device(): pl.pallas_call(store_kernel, out_shape=(jax.ShapeDtypeStruct(block, f32),...  1.09 us

profile of v2, /device:TPU:0, one launch (start us, length us, event | category | flops | bytes accessed | tf_op | source)
XLA Modules:
  0.0 29.0 jit_solution(4661395180895698009)
XLA Ops:
  0.6 27.3 %md_step.1 = (f32[4,2,3,3,3,8,128]{6,5,4,3,2,1,0:T(8,128)S(1)}, f32[4,2,3,3,2,8,128]{6,5,4,3,2,1,0:T(8,128)S(1)}, f32[8,128]{1,0:T(8,128)S(1)}) custom-call(f32[4,2,3,3,2,8,128]{6,5,4,3,2,1,0:T(8,128)} %links_in.1, f32[4,2,3,3,2,8,128]{6,5,4,3,2,1,0:T(8,128)} %mom_in.1), custom_call_target="tpu_custom_call" | custom-call | tf_op jit(solution)/shard_map/md_step/pallas_call | solution.py:591
  27.9 1.1 %store.1 = (f32[4,2,3,3,2,8,128]{6,5,4,3,2,1,0:T(8,128)}, f32[4,2,3,3,2,8,128]{6,5,4,3,2,1,0:T(8,128)}, f32[1,128]{1,0:T(1,128)}) custom-call(f32[4,2,3,3,3,8,128]{6,5,4,3,2,1,0:T(8,128)S(1)} %get-tuple-element.9.links, f32[4,2,3,3,2,8,128]{6,5,4,3,2,1,0:T(8,128)S(1)} %get-tuple-element.10.mom, f32[8,128]{1,0:T(8,128)S(1)} %get-tuple-element.11.plaq), custom_call_target="tpu_custom_call" | custom-call | tf_op jit(solution)/shard_map/store/pallas_call | solution.py:638

commit v3 on v2

--- a/solution.py
+++ b/solution.py
@@ -133,12 +133,11 @@
     ZBR,
     TR,
     load_sem,
-    fsend,
+    send_sem,
     frecv,
-    bsend,
     brecv,
-    tsend,
     trecv,
+    lines,
     *slots,
 ):
     coords = [lax.axis_index(axis) for axis in AXES]
@@ -182,25 +181,40 @@
 
     pending = []
 
-    def send(src, dst, offset, send_sem, recv_sem):
+    def send(src, dst, offset, recv_sem):
         copy = pltpu.make_async_remote_copy(
             src_ref=src,
             dst_ref=dst,
-            send_sem=send_sem,
+            send_sem=send_sem.at[0],
             recv_sem=recv_sem,
             device_id=device(offset),
             device_id_type=MESH_ID,
         )
         copy.start()
-        pending.append(copy)
+        pending.append(rows_of(src))
         return copy
 
+    def rows_of(ref):
+        size = 1
+        for extent in ref.shape:
+            size *= extent
+        return size // 128
+
+    def wait_rows(count, sem):
+        part = lines.at[0:count]
+        pltpu.make_async_copy(part, part, sem).wait()
+
+    lane_of = {}
+    for d in range(3):
+        for m in range(4):
+            if d != m:
+                lane_of[d, m] = len(lane_of)
     forward = {}
     backward = {}
 
     def forward_send(stage, d, m, src, dst):
         forward[stage, d, m] = send(
-            src, dst, along(d, -1), fsend.at[stage, d, m], frecv.at[stage, d, m]
+            src, dst, along(d, -1), frecv.at[lane_of[d, m]]
         )
 
     def send_link(m):
@@ -260,7 +274,8 @@
             second = LB[stage, 2, m, :, 2]
             ZBS[stage, m] = choose(low, pltpu.roll(first, half_lanes, 2), second)
             src, dst = ZBS.at[stage, m], ZBR.at[stage, m]
-        backward[stage, d, m] = send(src, dst, along(d, 1), bsend.at[stage, d, m], brecv.at[stage, d, m])
+        send(src, dst, along(d, 1), brecv.at[m])
+        backward[stage, m] = backward.get((stage, m), 0) + rows_of(src)
 
     def ahead(stage, buf, n, d, x):
         rows = []
@@ -464,11 +479,8 @@
             NM[m, 1, j, i, x] = v[c + 1]
 
     def for_x(body):
-        def step(x, carry):
+        for x in range(2):
             body(x)
-            return carry
-
-        lax.fori_loop(0, 2, step, 0)
 
     def pairs_of(stage, buf):
         for m, n in PAIRS:
@@ -486,9 +498,7 @@
                 send_back(stage, d, link)
 
     def wait_back(stage, m):
-        for d in range(3):
-            if d != m:
-                backward[stage, d, m].wait_recv()
+        wait_rows(backward[stage, m], brecv.at[m])
 
     for position, m in enumerate((3, 0, 1, 2)):
         loads[position].wait()
@@ -519,22 +529,11 @@
         for axis in groups[index]:
             position = position * sizes[axis] + coords[axis]
         buf[position] = jnp.sum(value, axis=0, keepdims=True)
-        copies = []
-        for k, offset in enumerate(offsets(groups[index])):
-            copies.append(
-                send(
-                    buf.at[position],
-                    buf.at[position],
-                    offset,
-                    tsend.at[index, k],
-                    trecv.at[index, k],
-                )
-            )
-        return copies
-
-    def gathered(index, copies):
-        for copy in copies:
-            copy.wait_recv()
+        for offset in offsets(groups[index]):
+            send(buf.at[position], buf.at[position], offset, trecv.at[index])
+
+    def gathered(index):
+        wait_rows(slots[index].shape[0] - 1, trecv.at[index])
         value = slots[index][0]
         for k in range(1, slots[index].shape[0]):
             value = value + slots[index][k]
@@ -546,26 +545,24 @@
         for_x(lambda x: last_update(m, x))
 
     value = TR[0] + TR[1]
-    copies = spread(0, value)
+    spread(0, value)
     for position, m in enumerate(UPDATES):
         finish(m)
         if position + 1 < len(groups):
-            value = gathered(position, copies)
-            copies = spread(position + 1, value)
+            value = gathered(position)
+            spread(position + 1, value)
     with jax.named_scope("plaq"):
-        lanes = gathered(len(groups) - 1, copies) * (4.0 / (72.0 * volume))
+        lanes = gathered(len(groups) - 1) * (4.0 / (72.0 * volume))
         plaq_out[...] = jnp.broadcast_to(jnp.sum(lanes, axis=1, keepdims=True), (8, 128))
-    for copy in pending:
-        copy.wait_send()
+    wait_rows(sum(pending), send_sem.at[0])
 
 
 def store_kernel(links, mom, plaq, links_out, mom_out, plaq_out, sem):
-    copies = [pltpu.make_async_copy(plaq.at[0:1], plaq_out, sem.at[8])]
-    for m in range(4):
-        copies.append(
-            pltpu.make_async_copy(links.at[m, :, :, :, 0:2], links_out.at[m], sem.at[m])
-        )
-        copies.append(pltpu.make_async_copy(mom.at[m], mom_out.at[m], sem.at[4 + m]))
+    copies = [
+        pltpu.make_async_copy(links.at[:, :, :, :, 0:2], links_out, sem.at[0]),
+        pltpu.make_async_copy(mom, mom_out, sem.at[1]),
+        pltpu.make_async_copy(plaq.at[0:1], plaq_out, sem.at[2]),
+    ]
     for copy in copies:
         copy.start()
     for copy in copies:
@@ -622,12 +619,11 @@
             vm(2, 4, 8, 8, 128),
             vm(2, 8, 128),
             dma((5,)),
-            dma((2, 3, 4)),
-            dma((2, 3, 4)),
-            dma((2, 3, 4)),
-            dma((2, 3, 4)),
-            dma((len(groups), max(counts))),
-            dma((len(groups), max(counts))),
+            dma((1,)),
+            dma((9,)),
+            dma((4,)),
+            dma((len(groups),)),
+            vm(8192, 1, 128),
             *[vm(count, 1, 128) for count in counts],
         ],
         compiler_params=pltpu.CompilerParams(collective_id=0, has_side_effects=True),
@@ -644,7 +640,7 @@
         ),
         in_specs=[in_vmem] * 3,
         out_specs=(anywhere,) * 3,
-        scratch_shapes=[dma((9,))],
+        scratch_shapes=[dma((3,))],
         name="store",
     )(
         pltpu.with_memory_space_constraint(wide_links, pltpu.VMEM),

time: 29.1 us -> 26.8 us (0.921)
  Pallas kernels: 28.4 us -> 26 us
    pallas_call x1, Pallas kernels: 27.3 us -> 24.9 us  [per_device(): pl.pallas_call(functools.partial(kernel, sizes, volume, groups), out_shap...]
where the time goes in v3:
time: 26.8 us; the launch traced here: 26.6 us
  Pallas kernels  26 us (97%)
  between operations  0.64 us (2%)
    pallas_call x1, Pallas kernels, per_device(): pl.pallas_call(functools.partial(kernel, sizes, volume, groups), out_shap...  24.9 us
    pallas_call x1, Pallas kernels, per_device(): pl.pallas_call(store_kernel, out_shape=(jax.ShapeDtypeStruct(block, f32),...  1.04 us

profile of v3, /device:TPU:0, one launch (start us, length us, event | category | flops | bytes accessed | tf_op | source)
XLA Modules:
  0.0 26.6 jit_solution(12422623282687040460)
XLA Ops:
  0.6 24.9 %md_step.1 = (f32[4,2,3,3,3,8,128]{6,5,4,3,2,1,0:T(8,128)S(1)}, f32[4,2,3,3,2,8,128]{6,5,4,3,2,1,0:T(8,128)S(1)}, f32[8,128]{1,0:T(8,128)S(1)}) custom-call(f32[4,2,3,3,2,8,128]{6,5,4,3,2,1,0:T(8,128)} %links_in.1, f32[4,2,3,3,2,8,128]{6,5,4,3,2,1,0:T(8,128)} %mom_in.1), custom_call_target="tpu_custom_call" | custom-call | tf_op jit(solution)/shard_map/md_step/pallas_call | solution.py:588
  25.6 1.0 %store.1 = (f32[4,2,3,3,2,8,128]{6,5,4,3,2,1,0:T(8,128)}, f32[4,2,3,3,2,8,128]{6,5,4,3,2,1,0:T(8,128)}, f32[1,128]{1,0:T(1,128)}) custom-call(f32[4,2,3,3,3,8,128]{6,5,4,3,2,1,0:T(8,128)S(1)} %get-tuple-element.9.links, f32[4,2,3,3,2,8,128]{6,5,4,3,2,1,0:T(8,128)S(1)} %get-tuple-element.10.mom, f32[8,128]{1,0:T(8,128)S(1)} %get-tuple-element.11.plaq), custom_call_target="tpu_custom_call" | custom-call | tf_op jit(solution)/shard_map/store/pallas_call | solution.py:634

commit v4 on v3

--- a/solution.py
+++ b/solution.py
@@ -10,6 +10,11 @@
 LT = 64
 AXES = ("gx", "gy", "zt")
 PAIRS = ((1, 3), (0, 3), (0, 1), (2, 3), (0, 2), (1, 2))
+ORDERS = (
+    ((0, 3), (2, 3), (1, 3), (0, 1), (1, 2), (0, 2)),
+    ((0, 3), (1, 3), (2, 3), (0, 2), (0, 1), (1, 2)),
+)
+EARLY = 1
 UPDATES = (3, 0, 2, 1)
 MESH_ID = pl.DeviceIdType.MESH
 
@@ -217,34 +222,35 @@
             src, dst, along(d, -1), frecv.at[lane_of[d, m]]
         )
 
-    def send_link(m):
-        for d in (2, 0, 1):
-            if d == m:
-                continue
-            if d == 0:
-                src, dst = V.at[m, :, :, :, 0], V.at[m, :, :, :, 2]
-            elif d == 1:
-                for r in range(2):
-                    for i in range(3):
-                        for x in range(2):
-                            YS[m, r, i, :, x : x + 1] = V[m, r, i, :, x, 0:1, :]
-                src, dst = YS.at[m], YR.at[0, m]
-            else:
-                rows = []
-                for i in range(3):
-                    parts = []
-                    for r in range(2):
-                        first = V[m, r, i, :, 0]
-                        second = V[m, r, i, :, 1]
-                        parts.append(choose(low, first, pltpu.roll(second, half_lanes, 2)))
-                    rows.append(tuple(parts))
-                for c, value in enumerate(encode(rows)):
-                    ZS[m, c] = value
-                src, dst = ZS.at[m], ZR.at[m]
-            forward_send(0, d, m, src, dst)
+    def pack_y(m):
+        for r in range(2):
+            for i in range(3):
+                for x in range(2):
+                    YS[m, r, i, :, x : x + 1] = V[m, r, i, :, x, 0:1, :]
+
+    def pack_z(m):
+        rows = []
+        for i in range(3):
+            parts = []
+            for r in range(2):
+                first = V[m, r, i, :, 0]
+                second = V[m, r, i, :, 1]
+                parts.append(choose(low, first, pltpu.roll(second, half_lanes, 2)))
+            rows.append(tuple(parts))
+        for c, value in enumerate(encode(rows)):
+            ZS[m, c] = value
+
+    def send_link(d, m):
+        if d == 0:
+            src, dst = V.at[m, :, :, :, 0], V.at[m, :, :, :, 2]
+        elif d == 1:
+            src, dst = YS.at[m], YR.at[0, m]
+        else:
+            src, dst = ZS.at[m], ZR.at[m]
+        forward_send(0, d, m, src, dst)
 
     def send_half(m):
-        for d in (2, 0, 1):
+        for d in (1, 2, 0):
             if d == m:
                 continue
             if d == 0:
@@ -338,7 +344,7 @@
         r12 = total([mul_conj_first(pick(rows[k], 1), pick(M[k], 2)) for k in range(3)])
         return [r0, r1, row0[0][0], row0[1][0], row0[0][1], row0[1][1], r12[0], r12[1]]
 
-    def pair_task(stage, buf, m, n, x):
+    def loop_task(stage, buf, m, n, x):
         index = PAIRS.index((m, n))
         n_ahead = ahead(stage, buf, n, m, x)
         A = []
@@ -373,8 +379,15 @@
             TB[index, c, x] = values[c]
         if stage == 1:
             trace = loop[0][0][0] + loop[1][0][1] + loop[2][0][2]
-            TR[x] = trace if index == 0 else TR[x] + trace
-        T = (d0, d1, d2, h01, h02, h12)
+            TR[x] = trace if (m, n) == ORDERS[1][0] else TR[x] + trace
+        return values
+
+    def staple_task(stage, buf, m, n, x, values=None):
+        if values is None:
+            index = PAIRS.index((m, n))
+            values = [TB[index, c, x] for c in range(8)]
+        d0, d1 = values[0], values[1]
+        T = (d0, d1, -(d0 + d1), tuple(values[2:4]), tuple(values[4:6]), tuple(values[6:8]))
         for link, d in ((m, n), (n, m)):
             rows = [(buf[d, 0, k, :, x], buf[d, 1, k, :, x]) for k in range(3)]
             result = conjugate(T, rows)
@@ -482,39 +495,60 @@
         for x in range(2):
             body(x)
 
-    def pairs_of(stage, buf):
-        for m, n in PAIRS:
-            for link, d in ((n, m), (m, n)):
-                if d == 3:
-                    continue
-                with jax.named_scope(f"wf{stage}_d{d}m{link}"):
-                    forward[stage, d, link].wait_recv()
-                if stage == 1:
-                    halo_update(d, link)
-                elif d == 2:
-                    halo_decode(link)
-            for_x(lambda x: pair_task(stage, buf, m, n, x))
-            for link, d in ((m, n), (n, m)):
-                send_back(stage, d, link)
+    def wait_ahead(stage, m, n):
+        for link, d in ((n, m), (m, n)):
+            if d == 3:
+                continue
+            with jax.named_scope(f"wf{stage}_d{d}m{link}"):
+                forward[stage, d, link].wait_recv()
+            if stage == 1:
+                halo_update(d, link)
+            elif d == 2:
+                halo_decode(link)
+
+    def send_pair(stage, m, n):
+        for link, d in ((m, n), (n, m)):
+            send_back(stage, d, link)
+
+    def whole_pair(stage, buf, m, n):
+        wait_ahead(stage, m, n)
+        for_x(lambda x: staple_task(stage, buf, m, n, x, loop_task(stage, buf, m, n, x)))
+        send_pair(stage, m, n)
 
     def wait_back(stage, m):
         wait_rows(backward[stage, m], brecv.at[m])
 
-    for position, m in enumerate((3, 0, 1, 2)):
-        loads[position].wait()
-        if position == 0:
-            with jax.named_scope("bar"):
-                pl.semaphore_wait(barrier, partners)
-        send_link(m)
-    pairs_of(0, V)
+    for copy in loads:
+        copy.wait()
+    for m in (3, 0, 2):
+        pack_y(m)
+    with jax.named_scope("bar"):
+        pl.semaphore_wait(barrier, partners)
+    for d, m in ((1, 3), (0, 3), (1, 0), (1, 2)):
+        send_link(d, m)
+    pack_z(3)
+    for d, m in ((2, 3), (0, 1), (0, 2)):
+        send_link(d, m)
+    for m in (1, 0):
+        pack_z(m)
+        send_link(2, m)
+    for m, n in ORDERS[0]:
+        whole_pair(0, V, m, n)
     mom_load.wait()
     for m in UPDATES:
         with jax.named_scope(f"wb0_{m}"):
             wait_back(0, m)
         for_x(lambda x: half_update(m, x))
         send_half(m)
+        if m == UPDATES[2]:
+            for_x(lambda x: link_update(UPDATES[0], x))
+    for m in UPDATES[1:]:
         for_x(lambda x: link_update(m, x))
-    pairs_of(1, W)
+    for m, n in ORDERS[1][:EARLY]:
+        whole_pair(1, W, m, n)
+    for m, n in ORDERS[1][EARLY:]:
+        wait_ahead(1, m, n)
+        for_x(lambda x: loop_task(1, W, m, n, x))
 
     def offsets(group):
         result = [()]
@@ -546,6 +580,9 @@
 
     value = TR[0] + TR[1]
     spread(0, value)
+    for m, n in ORDERS[1][EARLY:]:
+        for_x(lambda x: staple_task(1, W, m, n, x))
+        send_pair(1, m, n)
     for position, m in enumerate(UPDATES):
         finish(m)
         if position + 1 < len(groups):

time: 26.8 us -> 25.4 us (0.948)
  Pallas kernels: 26 us -> 24.6 us
    pallas_call x1, Pallas kernels: 24.9 us -> 23.6 us  [per_device(): pl.pallas_call(functools.partial(kernel, sizes, volume, groups), out_shap...]
where the time goes in v4:
time: 25.4 us; the launch traced here: 25.3 us
  Pallas kernels  24.6 us (97%)
  between operations  0.64 us (3%)
    pallas_call x1, Pallas kernels, per_device(): pl.pallas_call(functools.partial(kernel, sizes, volume, groups), out_shap...  23.6 us
    pallas_call x1, Pallas kernels, per_device(): pl.pallas_call(store_kernel, out_shape=(jax.ShapeDtypeStruct(block, f32),...  1.04 us

profile of v4, /device:TPU:0, one launch (start us, length us, event | category | flops | bytes accessed | tf_op | source)
XLA Modules:
  0.0 25.3 jit_solution(8015582776287739336)
XLA Ops:
  0.6 23.6 %md_step.1 = (f32[4,2,3,3,3,8,128]{6,5,4,3,2,1,0:T(8,128)S(1)}, f32[4,2,3,3,2,8,128]{6,5,4,3,2,1,0:T(8,128)S(1)}, f32[8,128]{1,0:T(8,128)S(1)}) custom-call(f32[4,2,3,3,2,8,128]{6,5,4,3,2,1,0:T(8,128)} %links_in.1, f32[4,2,3,3,2,8,128]{6,5,4,3,2,1,0:T(8,128)} %mom_in.1), custom_call_target="tpu_custom_call" | custom-call | tf_op jit(solution)/shard_map/md_step/pallas_call | solution.py:625
  24.2 1.0 %store.1 = (f32[4,2,3,3,2,8,128]{6,5,4,3,2,1,0:T(8,128)}, f32[4,2,3,3,2,8,128]{6,5,4,3,2,1,0:T(8,128)}, f32[1,128]{1,0:T(1,128)}) custom-call(f32[4,2,3,3,3,8,128]{6,5,4,3,2,1,0:T(8,128)S(1)} %get-tuple-element.9.links, f32[4,2,3,3,2,8,128]{6,5,4,3,2,1,0:T(8,128)S(1)} %get-tuple-element.10.mom, f32[8,128]{1,0:T(8,128)S(1)} %get-tuple-element.11.plaq), custom_call_target="tpu_custom_call" | custom-call | tf_op jit(solution)/shard_map/store/pallas_call | solution.py:671

commit v5 on v4

--- a/solution.py
+++ b/solution.py
@@ -11,11 +11,15 @@
 AXES = ("gx", "gy", "zt")
 PAIRS = ((1, 3), (0, 3), (0, 1), (2, 3), (0, 2), (1, 2))
 ORDERS = (
-    ((0, 3), (2, 3), (1, 3), (0, 1), (1, 2), (0, 2)),
-    ((0, 3), (1, 3), (2, 3), (0, 2), (0, 1), (1, 2)),
+    ((1, 3), (0, 3), (0, 1), (2, 3), (1, 2), (0, 2)),
+    ((1, 3), (2, 3), (0, 3), (0, 2), (0, 1), (1, 2)),
 )
-EARLY = 1
-UPDATES = (3, 0, 2, 1)
+EARLY = 2
+EDGE = (3, 0, 2)
+LOADS = (3, 1, 0, 2)
+Z_LINKS = (3, 0, 1)
+SENDS = ((0, 3), (2, 3), (1, 3), (2, 1), (0, 1), (2, 0), (1, 0), (0, 2), (1, 2))
+UPDATES = (3, 0, 1, 2)
 MESH_ID = pl.DeviceIdType.MESH
 
 kick_size = 0.25
@@ -56,6 +60,8 @@
 TINY = 1e-30
 FAR = 1e15
 CODED = 11
+LANES = 15
+CODED_X = (1, 2)
 
 
 def project(first, rest):
@@ -123,16 +129,21 @@
     HB,
     TB,
     LB,
-    YS,
-    YR,
+    XS,
+    XR,
+    EM,
+    EN,
     YHS,
-    YHR,
+    EX,
+    EP,
+    EH,
+    EK,
+    ET,
     ZS,
     ZR,
     ZHS,
     ZHR,
     ZL,
-    YBS,
     YBR,
     ZBS,
     ZBR,
@@ -156,7 +167,7 @@
         return tuple(distance if other == axis else 0 for other in range(3))
 
     loads = []
-    for m in (3, 0, 1, 2):
+    for m in LOADS:
         copy = pltpu.make_async_copy(links_in.at[m], V.at[m, :, :, :, 0:2], load_sem.at[m])
         copy.start()
         loads.append(copy)
@@ -173,12 +184,13 @@
     shape3 = (1, 8, 128)
     lane = lax.broadcasted_iota(jnp.int32, shape3, 2)
     sub = lax.broadcasted_iota(jnp.int32, shape3, 1)
+    sub2 = lax.broadcasted_iota(jnp.int32, shape3[1:], 0)
     t_index = lax.rem(lane, LT)
     half_lanes = lane.shape[-1] // 2
     low = lane < half_lanes
+    low_row = lax.broadcasted_iota(jnp.int32, (1, 1, 128), 2) < half_lanes
     t_last = t_index == LT - 1
     t_first = t_index == 0
-    y_last = sub == 7
     y_first = sub == 0
 
     def choose(mask, a, b):
@@ -213,20 +225,26 @@
     for d in range(3):
         for m in range(4):
             if d != m:
-                lane_of[d, m] = len(lane_of)
+                lane_of[0, d, m] = len(set(lane_of.values()))
+                lane_of[1, d, m] = lane_of[0, d, m] + (d > 0)
     forward = {}
     backward = {}
 
     def forward_send(stage, d, m, src, dst):
-        forward[stage, d, m] = send(
-            src, dst, along(d, -1), frecv.at[lane_of[d, m]]
-        )
-
-    def pack_y(m):
-        for r in range(2):
-            for i in range(3):
-                for x in range(2):
-                    YS[m, r, i, :, x : x + 1] = V[m, r, i, :, x, 0:1, :]
+        send(src, dst, along(d, -1), frecv.at[lane_of[stage, d, m]])
+        forward[stage, d, m] = forward.get((stage, d, m), 0) + rows_of(src)
+
+    def wait_forward(stage, d, m):
+        with jax.named_scope(f"wf{stage}_d{d}m{m}"):
+            wait_rows(forward[stage, d, m], frecv.at[lane_of[stage, d, m]])
+
+    def edge_row(m, x):
+        row = 2 * EDGE.index(m) + x
+        return slice(row, row + 1)
+
+    def store_code(buf, m, rows):
+        for c, value in enumerate(encode(rows)):
+            buf[m, c] = value
 
     def pack_z(m):
         rows = []
@@ -237,51 +255,78 @@
                 second = V[m, r, i, :, 1]
                 parts.append(choose(low, first, pltpu.roll(second, half_lanes, 2)))
             rows.append(tuple(parts))
-        for c, value in enumerate(encode(rows)):
-            ZS[m, c] = value
+        store_code(ZS, m, rows)
 
     def send_link(d, m):
-        if d == 0:
-            src, dst = V.at[m, :, :, :, 0], V.at[m, :, :, :, 2]
-        elif d == 1:
-            src, dst = YS.at[m], YR.at[0, m]
+        if d == 1:
+            for x in range(2):
+                forward_send(0, 1, m, V.at[m, :, :, :, x, 0:1], EH.at[:, :, :, edge_row(m, x)])
+        elif d == 2:
+            pack_z(m)
+            forward_send(0, 2, m, ZS.at[m], ZR.at[m])
+        elif m in CODED_X:
+            store_code(XS, m, [(V[m, 0, k, :, 0], V[m, 1, k, :, 0]) for k in range(3)])
+            forward_send(0, 0, m, XS.at[m], XR.at[m])
         else:
-            src, dst = ZS.at[m], ZR.at[m]
-        forward_send(0, d, m, src, dst)
-
-    def send_half(m):
-        for d in (1, 2, 0):
-            if d == m:
-                continue
-            if d == 0:
-                src, dst = HB.at[m, :, 0], HB.at[m, :, 2]
-            elif d == 1:
-                for x in range(2):
-                    YHS[m, :, x : x + 1] = HB[m, :, x, 0:1, :]
-                src, dst = YHS.at[m], YHR.at[m]
-            else:
-                first = HB[m, :, 0]
-                second = HB[m, :, 1]
-                ZHS[m] = choose(low, first, pltpu.roll(second, half_lanes, 2))
-                src, dst = ZHS.at[m], ZHR.at[m]
-            forward_send(1, d, m, src, dst)
+            forward_send(0, 0, m, V.at[m, :, :, :, 0], V.at[m, :, :, :, 2])
+
+    def share(d, m):
+        return (0.5 * kick_size) if m < d else (-0.5 * kick_size)
+
+    def add_x(m):
+        if m != 0:
+            wait_back(0, m, (0,))
+            HB[m, :, 0] = HB[m, :, 0] + share(0, m) * LB[0, 0, m, :, 0]
+
+    def add_y(m):
+        if m != 1:
+            if m == 2:
+                wait_back(0, m, (1,))
+            for x in range(2):
+                HB[m, :, x, 0:1] = HB[m, :, x, 0:1] + share(1, m) * YBR[0, m, :, x]
+
+    def add_z(m):
+        if m == 2:
+            return
+        wait_back(0, m, (2,))
+        for x in range(2):
+            halo = pltpu.roll(ZBR[0, m], half_lanes * x, 2) if x else ZBR[0, m]
+            HB[m, :, x] = HB[m, :, x] + choose(low, share(2, m) * halo, jnp.zeros_like(halo))
+
+    def send_half_z(m):
+        ZHS[m] = choose(low, HB[m, :, 0], pltpu.roll(HB[m, :, 1], half_lanes, 2))
+        if m != 1:
+            wait_back(0, m, (1,))
+            first, second = YBR[0, m, :, 0], YBR[0, m, :, 1]
+            row = choose(low_row, first, pltpu.roll(second, half_lanes, 2))
+            ZHS[m, :, 0:1] = ZHS[m, :, 0:1] + share(1, m) * row
+        forward_send(1, 2, m, ZHS.at[m], ZHR.at[m])
+
+    def send_half_y(m):
+        if m != 1:
+            for x in range(2):
+                YHS[m, :, x] = HB[m, :, x, 0:1]
+                forward_send(1, 1, m, YHS.at[m, :, x], EK.at[:, edge_row(m, x)])
+
+    def send_half_x(m):
+        if m != 0:
+            forward_send(1, 0, m, HB.at[m, :, 0], HB.at[m, :, 2])
 
     def send_back(stage, d, m):
         if d == 3:
             return
         if d == 0:
-            src, dst = LB.at[stage, 0, m, :, 2], LB.at[stage, 0, m, :, 0]
+            copies = [(LB.at[stage, 0, m, :, 2], LB.at[stage, 0, m, :, 0])]
         elif d == 1:
-            for x in range(2):
-                YBS[stage, m, :, x] = LB[stage, 1, m, :, x + 1, 7:8, :]
-            src, dst = YBS.at[stage, m], YBR.at[stage, m]
+            copies = [(ET.at[stage, 1, :, edge_row(m, x)], YBR.at[stage, m, :, x]) for x in range(2)]
         else:
             first = LB[stage, 2, m, :, 1]
             second = LB[stage, 2, m, :, 2]
             ZBS[stage, m] = choose(low, pltpu.roll(first, half_lanes, 2), second)
-            src, dst = ZBS.at[stage, m], ZBR.at[stage, m]
-        send(src, dst, along(d, 1), brecv.at[m])
-        backward[stage, m] = backward.get((stage, m), 0) + rows_of(src)
+            copies = [(ZBS.at[stage, m], ZBR.at[stage, m])]
+        for src, dst in copies:
+            send(src, dst, along(d, 1), brecv.at[lane_of[stage, d, m]])
+            backward[stage, d, m] = backward.get((stage, d, m), 0) + rows_of(src)
 
     def ahead(stage, buf, n, d, x):
         rows = []
@@ -297,8 +342,7 @@
                         choose(t_last, pltpu.roll(value, LT - 1, 2), pltpu.roll(value, 127, 2))
                     )
                 elif d == 1:
-                    row = YR[stage, n, r, k, :, pl.ds(x, 1)]
-                    parts.append(choose(y_last, row, pltpu.roll(value, 7, 1)))
+                    parts.append(pltpu.roll(value, 7, 1))
                 else:
                     halo = pltpu.roll(ZL[stage, n, r, k], half_lanes * (1 - x), 2)
                     parts.append(choose(low, pltpu.roll(value, half_lanes, 2), halo))
@@ -344,6 +388,27 @@
         r12 = total([mul_conj_first(pick(rows[k], 1), pick(M[k], 2)) for k in range(3)])
         return [r0, r1, row0[0][0], row0[1][0], row0[0][1], row0[1][1], r12[0], r12[1]]
 
+    def close(A, m_ahead, columns):
+        Bt = []
+        for k in range(3):
+            Bt.append(total([mul(pick(m_ahead[l], k), columns[l]) for l in range(3)]))
+        loop = []
+        for i in range(3):
+            loop.append(total([mul_conj_second(pick(A[i], k), Bt[k]) for k in range(3)]))
+        i0, i1, i2 = loop[0][1][0], loop[1][1][1], loop[2][1][2]
+        mean = (i0 + i1 + i2) * (2.0 / 3.0)
+        d0 = 2.0 * i0 - mean
+        d1 = 2.0 * i1 - mean
+
+        def off(i, j):
+            a = pick(loop[i], j)
+            b = pick(loop[j], i)
+            return a[0] - b[0], a[1] + b[1]
+
+        h01, h02, h12 = off(0, 1), off(0, 2), off(1, 2)
+        values = [d0, d1, h01[0], h01[1], h02[0], h02[1], h12[0], h12[1]]
+        return values, loop[0][0][0] + loop[1][0][1] + loop[2][0][2]
+
     def loop_task(stage, buf, m, n, x):
         index = PAIRS.index((m, n))
         n_ahead = ahead(stage, buf, n, m, x)
@@ -356,51 +421,98 @@
             )
         m_ahead = ahead(stage, buf, m, n, x)
         columns = [(buf[n, 0, :, l, x], buf[n, 1, :, l, x]) for l in range(3)]
-        Bt = []
-        for k in range(3):
-            Bt.append(total([mul(pick(m_ahead[l], k), columns[l]) for l in range(3)]))
-        loop = []
-        for i in range(3):
-            loop.append(total([mul_conj_second(pick(A[i], k), Bt[k]) for k in range(3)]))
-        i0, i1, i2 = loop[0][1][0], loop[1][1][1], loop[2][1][2]
-        mean = (i0 + i1 + i2) * (2.0 / 3.0)
-        d0 = 2.0 * i0 - mean
-        d1 = 2.0 * i1 - mean
-        d2 = -(d0 + d1)
-
-        def off(i, j):
-            a = pick(loop[i], j)
-            b = pick(loop[j], i)
-            return a[0] - b[0], a[1] + b[1]
-
-        h01, h02, h12 = off(0, 1), off(0, 2), off(1, 2)
-        values = [d0, d1, h01[0], h01[1], h02[0], h02[1], h12[0], h12[1]]
+        values, trace = close(A, m_ahead, columns)
         for c in range(8):
             TB[index, c, x] = values[c]
         if stage == 1:
-            trace = loop[0][0][0] + loop[1][0][1] + loop[2][0][2]
+            if 1 in (m, n):
+                trace = jnp.where(sub2 == 7, 0.0, trace)
             TR[x] = trace if (m, n) == ORDERS[1][0] else TR[x] + trace
         return values
+
+    def algebra(values):
+        d0, d1 = values[0], values[1]
+        return (d0, d1, -(d0 + d1), tuple(values[2:4]), tuple(values[4:6]), tuple(values[6:8]))
+
+    def edge_rows(stage, buf):
+        for r in range(2):
+            for k in range(3):
+                for s, m in enumerate(EDGE):
+                    for x in range(2):
+                        row = slice(2 * s + x, 2 * s + x + 1)
+                        EM[r, k, :, row] = buf[m, r, k, :, x, 7:8, :]
+                        EN[r, k, :, row] = buf[1, r, k, :, x, 7:8, :]
+                for x in range(2):
+                    EX[r, k, :, 2 + x : 3 + x] = buf[1, r, k, :, x + 1, 7:8, :]
+                    EX[r, k, :, 4 + x : 5 + x] = ZL[stage, 1, r, k, :, 7:8]
+        n_ahead = []
+        for k in range(3):
+            parts = []
+            for r in range(2):
+                own, other = EN[r, k], EX[r, k]
+                t_ahead = choose(t_last, pltpu.roll(own, LT - 1, 2), pltpu.roll(own, 127, 2))
+                halo = choose(sub == 4, pltpu.roll(other, half_lanes, 2), other)
+                z_ahead = choose(low, pltpu.roll(own, half_lanes, 2), halo)
+                parts.append(choose(sub < 2, t_ahead, choose(sub < 4, other, z_ahead)))
+            n_ahead.append(tuple(parts))
+        for i in range(3):
+            value = total([mul((EM[0, i, k], EM[1, i, k]), n_ahead[k]) for k in range(3)])
+            EP[0, i], EP[1, i] = value
+
+    def edge_loops(stage):
+        for m in EDGE:
+            wait_forward(stage, 1, m)
+        m_ahead = [(EH[0, k], EH[1, k]) for k in range(3)]
+        if stage == 1:
+            scale = jnp.where((sub2 < 2) | (sub2 > 3), share(1, 3), share(1, 0))
+            m_ahead = cayley([EK[c] + scale * ET[0, 1, c] for c in range(8)], m_ahead)
+        A = [(EP[0, i], EP[1, i]) for i in range(3)]
+        columns = [(EN[0, :, l], EN[1, :, l]) for l in range(3)]
+        values, trace = close(A, m_ahead, columns)
+        if stage == 1:
+            TR[0] = TR[0] + jnp.where(sub2 < 6, trace, 0.0)
+        sign = jnp.where((sub2 < 2) | (sub2 > 3), -1.0, 1.0)
+        for c in range(8):
+            ET[stage, 0, c] = sign * values[c]
+
+    def edge_staples(stage):
+        T = algebra([ET[stage, 0, c] for c in range(8)])
+        for slot, buf in ((1, EN), (2, EM)):
+            result = conjugate(T, [(buf[0, k], buf[1, k]) for k in range(3)])
+            for c in range(8):
+                ET[stage, slot, c] = result[c]
+        for m in EDGE:
+            send_back(stage, 1, m)
+
+    def edge_merge(stage):
+        for m in EDGE:
+            index = PAIRS.index((min(m, 1), max(m, 1)))
+            for x in range(2):
+                TB[index, :, x, 7:8] = ET[stage, 0, :, edge_row(m, x)]
+                LB[stage, m, 1, :, x + 1, 7:8] = ET[stage, 2, :, edge_row(m, x)]
+        for d in (2, 0):
+            send_back(stage, d, 1)
 
     def staple_task(stage, buf, m, n, x, values=None):
         if values is None:
             index = PAIRS.index((m, n))
             values = [TB[index, c, x] for c in range(8)]
-        d0, d1 = values[0], values[1]
-        T = (d0, d1, -(d0 + d1), tuple(values[2:4]), tuple(values[4:6]), tuple(values[6:8]))
+        T = algebra(values)
         for link, d in ((m, n), (n, m)):
             rows = [(buf[d, 0, k, :, x], buf[d, 1, k, :, x]) for k in range(3)]
             result = conjugate(T, rows)
             for c in range(8):
                 LB[stage, d, link, c, x + 1] = result[c]
 
-    def force(stage, m, x):
+    def force(stage, m, x, directions=(0, 1, 2, 3)):
         result = None
         for n in range(4):
             if n == m:
                 continue
             index = PAIRS.index((min(m, n), max(m, n)))
-            term = TB[index, :, x] - behind(stage, n, m, x)
+            term = TB[index, :, x]
+            if n in directions:
+                term = term - behind(stage, n, m, x)
             if result is None:
                 result = term if m < n else -term
             else:
@@ -410,7 +522,24 @@
     places = ((1, 0, 0), (1, 1, 1), (0, 0, 1), (1, 0, 1), (0, 0, 2), (1, 0, 2), (0, 1, 2), (1, 1, 2))
 
     def half_update(m, x):
-        F = force(0, m, x)
+        F = None
+        for n in range(4):
+            if n == m:
+                continue
+            term = TB[PAIRS.index((min(m, n), max(m, n))), :, x]
+            if n == 0 and x:
+                term = term - LB[0, 0, m, :, x]
+            elif n != 0:
+                value = LB[0, n, m, :, x + 1]
+                if n == 1:
+                    back = choose(y_first, jnp.zeros_like(value), pltpu.roll(value, 1, 1))
+                elif n == 2:
+                    back = choose(low, jnp.zeros_like(value), pltpu.roll(value, half_lanes, 2))
+                else:
+                    back = behind(0, 3, m, x)
+                term = term - back
+            term = term if m < n else -term
+            F = term if F is None else F + term
         for c, (r, i, j) in enumerate(places):
             HB[m, c, x] = MB[m, r, i, j, x] - (0.5 * kick_size) * F[c]
 
@@ -462,12 +591,12 @@
         if d == 0:
             link_update(m, 2)
             return
-        buf, momentum = (YR, YHR) if d == 1 else (ZL, ZHR)
-        rows = [(buf[0, m, 0, k], buf[0, m, 1, k]) for k in range(3)]
-        new = cayley([momentum[m, c] for c in range(8)], rows)
+        rows = [(ZL[0, m, 0, k], ZL[0, m, 1, k]) for k in range(3)]
+        scale = share(2, m)
+        new = cayley([ZHR[m, c] + scale * ZBS[0, m, c] for c in range(8)], rows)
         for i in range(3):
-            buf[1, m, 0, i] = new[i][0]
-            buf[1, m, 1, i] = new[i][1]
+            ZL[1, m, 0, i] = new[i][0]
+            ZL[1, m, 1, i] = new[i][1]
 
     def halo_decode(m):
         rows = decode([ZR[m, c] for c in range(CODED)])
@@ -497,16 +626,23 @@
 
     def wait_ahead(stage, m, n):
         for link, d in ((n, m), (m, n)):
-            if d == 3:
+            if d in (1, 3):
                 continue
-            with jax.named_scope(f"wf{stage}_d{d}m{link}"):
-                forward[stage, d, link].wait_recv()
+            wait_forward(stage, d, link)
             if stage == 1:
                 halo_update(d, link)
             elif d == 2:
                 halo_decode(link)
+            elif link in CODED_X:
+                rows = decode([XR[link, c] for c in range(CODED)])
+                for k in range(3):
+                    for r in range(2):
+                        for l in range(3):
+                            V[link, r, k, l, 2] = rows[k][l][r]
 
     def send_pair(stage, m, n):
+        if 1 in (m, n):
+            return
         for link, d in ((m, n), (n, m)):
             send_back(stage, d, link)
 
@@ -515,40 +651,51 @@
         for_x(lambda x: staple_task(stage, buf, m, n, x, loop_task(stage, buf, m, n, x)))
         send_pair(stage, m, n)
 
-    def wait_back(stage, m):
-        wait_rows(backward[stage, m], brecv.at[m])
-
-    for copy in loads:
-        copy.wait()
-    for m in (3, 0, 2):
-        pack_y(m)
+    def wait_back(stage, m, directions=(0, 1, 2)):
+        for d in directions:
+            if d != m:
+                with jax.named_scope(f"wb{stage}_d{d}m{m}"):
+                    wait_rows(backward[stage, d, m], brecv.at[lane_of[stage, d, m]])
+
+    waits = {m: position for position, m in enumerate(LOADS)}
+    loads[waits.pop(3)].wait()
     with jax.named_scope("bar"):
         pl.semaphore_wait(barrier, partners)
-    for d, m in ((1, 3), (0, 3), (1, 0), (1, 2)):
+    send_link(*SENDS[0])
+    for d, m in SENDS[1:]:
+        if m in waits and d != 1:
+            loads[waits.pop(m)].wait()
         send_link(d, m)
-    pack_z(3)
-    for d, m in ((2, 3), (0, 1), (0, 2)):
-        send_link(d, m)
-    for m in (1, 0):
-        pack_z(m)
-        send_link(2, m)
     for m, n in ORDERS[0]:
         whole_pair(0, V, m, n)
+        if (m, n) == (1, 2):
+            edge_rows(0, V)
+            edge_loops(0)
+            edge_staples(0)
+            edge_merge(0)
     mom_load.wait()
     for m in UPDATES:
-        with jax.named_scope(f"wb0_{m}"):
-            wait_back(0, m)
         for_x(lambda x: half_update(m, x))
-        send_half(m)
-        if m == UPDATES[2]:
-            for_x(lambda x: link_update(UPDATES[0], x))
-    for m in UPDATES[1:]:
+
+    for m in Z_LINKS:
+        add_x(m)
+        send_half_z(m)
+    for m in UPDATES:
+        if m == 2:
+            add_x(m)
+        add_z(m)
+        send_half_y(m)
+        add_y(m)
+        send_half_x(m)
+    for m in UPDATES:
         for_x(lambda x: link_update(m, x))
     for m, n in ORDERS[1][:EARLY]:
         whole_pair(1, W, m, n)
     for m, n in ORDERS[1][EARLY:]:
         wait_ahead(1, m, n)
         for_x(lambda x: loop_task(1, W, m, n, x))
+    edge_rows(1, W)
+    edge_loops(1)
 
     def offsets(group):
         result = [()]
@@ -574,15 +721,16 @@
         return value
 
     def finish(m):
-        with jax.named_scope(f"wb1_{m}"):
-            wait_back(1, m)
+        wait_back(1, m)
         for_x(lambda x: last_update(m, x))
 
     value = TR[0] + TR[1]
     spread(0, value)
+    edge_staples(1)
     for m, n in ORDERS[1][EARLY:]:
         for_x(lambda x: staple_task(1, W, m, n, x))
         send_pair(1, m, n)
+    edge_merge(1)
     for position, m in enumerate(UPDATES):
         finish(m)
         if position + 1 < len(groups):
@@ -641,24 +789,29 @@
             vm(4, 8, 3, 8, 128),
             vm(6, 8, 2, 8, 128),
             vm(2, 4, 4, 8, 3, 8, 128),
-            vm(4, 2, 3, 3, 2, 128),
-            vm(2, 4, 2, 3, 3, 2, 128),
-            vm(4, 8, 2, 128),
-            vm(4, 8, 2, 128),
+            vm(4, CODED, 8, 128),
+            vm(4, CODED, 8, 128),
+            vm(2, 3, 3, 8, 128),
+            vm(2, 3, 3, 8, 128),
+            vm(4, 8, 2, 1, 128),
+            vm(2, 3, 3, 8, 128),
+            vm(2, 3, 3, 8, 128),
+            vm(2, 3, 3, 8, 128),
+            vm(8, 8, 128),
+            vm(2, 3, 8, 8, 128),
             vm(4, CODED, 8, 128),
             vm(4, CODED, 8, 128),
             vm(4, 8, 8, 128),
             vm(4, 8, 8, 128),
             vm(2, 4, 2, 3, 3, 8, 128),
             vm(2, 4, 8, 2, 1, 128),
-            vm(2, 4, 8, 2, 1, 128),
             vm(2, 4, 8, 8, 128),
             vm(2, 4, 8, 8, 128),
             vm(2, 8, 128),
             dma((5,)),
             dma((1,)),
-            dma((9,)),
-            dma((4,)),
+            dma((LANES,)),
+            dma((LANES,)),
             dma((len(groups),)),
             vm(8192, 1, 128),
             *[vm(count, 1, 128) for count in counts],

time: 25.4 us -> 25.3 us (level)
  no operation moved by 1% of the time
where the time goes in v5:
time: 25.3 us; the launch traced here: 25.1 us
  Pallas kernels  24.5 us (97%)
  between operations  0.64 us (3%)
    pallas_call x1, Pallas kernels, per_device(): pl.pallas_call(functools.partial(kernel, sizes, volume, groups), out_shap...  23.5 us
    pallas_call x1, Pallas kernels, per_device(): pl.pallas_call(store_kernel, out_shape=(jax.ShapeDtypeStruct(block, f32),...  1.04 us

profile of v5, /device:TPU:0, one launch (start us, length us, event | category | flops | bytes accessed | tf_op | source)
XLA Modules:
  0.0 25.1 jit_solution(9086528781829340841)
XLA Ops:
  0.6 23.5 %md_step.1 = (f32[4,2,3,3,3,8,128]{6,5,4,3,2,1,0:T(8,128)S(1)}, f32[4,2,3,3,2,8,128]{6,5,4,3,2,1,0:T(8,128)S(1)}, f32[8,128]{1,0:T(8,128)S(1)}) custom-call(f32[4,2,3,3,2,8,128]{6,5,4,3,2,1,0:T(8,128)} %links_in.1, f32[4,2,3,3,2,8,128]{6,5,4,3,2,1,0:T(8,128)} %mom_in.1), custom_call_target="tpu_custom_call" | custom-call | tf_op jit(solution)/shard_map/md_step/pallas_call | solution.py:773
  24.1 1.0 %store.1 = (f32[4,2,3,3,2,8,128]{6,5,4,3,2,1,0:T(8,128)}, f32[4,2,3,3,2,8,128]{6,5,4,3,2,1,0:T(8,128)}, f32[1,128]{1,0:T(1,128)}) custom-call(f32[4,2,3,3,3,8,128]{6,5,4,3,2,1,0:T(8,128)S(1)} %get-tuple-element.9.links, f32[4,2,3,3,2,8,128]{6,5,4,3,2,1,0:T(8,128)S(1)} %get-tuple-element.10.mom, f32[8,128]{1,0:T(8,128)S(1)} %get-tuple-element.11.plaq), custom_call_target="tpu_custom_call" | custom-call | tf_op jit(solution)/shard_map/store/pallas_call | solution.py:824

commit v6 on v5

--- a/solution.py
+++ b/solution.py
@@ -18,7 +18,7 @@
 EDGE = (3, 0, 2)
 LOADS = (3, 1, 0, 2)
 Z_LINKS = (3, 0, 1)
-SENDS = ((0, 3), (2, 3), (1, 3), (2, 1), (0, 1), (2, 0), (1, 0), (0, 2), (1, 2))
+SENDS = ((0, 3), (1, 3), (2, 3), (1, 0), (1, 2), (2, 1), (0, 1), (2, 0), (0, 2))
 UPDATES = (3, 0, 1, 2)
 MESH_ID = pl.DeviceIdType.MESH
 
@@ -663,7 +663,7 @@
         pl.semaphore_wait(barrier, partners)
     send_link(*SENDS[0])
     for d, m in SENDS[1:]:
-        if m in waits and d != 1:
+        if m in waits:
             loads[waits.pop(m)].wait()
         send_link(d, m)
     for m, n in ORDERS[0]:
@@ -702,7 +702,8 @@
         for axis in range(3):
             span = range(sizes[axis]) if axis in group else (0,)
             result = [head + (k,) for head in result for k in span]
-        return [item for item in result if any(item)]
+        weight = lambda item: sum(min(k, size - k) + (k % 2) for k, size in zip(item, sizes))
+        return sorted([item for item in result if any(item)], key=weight, reverse=True)
 
     def spread(index, value):
         buf = slots[index]

time: 25.3 us -> 25.2 us (level)
  no operation moved by 1% of the time
where the time goes in v6:
time: 25.2 us; the launch traced here: 25 us
  Pallas kernels  24.4 us (97%)
  between operations  0.64 us (3%)
    pallas_call x1, Pallas kernels, per_device(): pl.pallas_call(functools.partial(kernel, sizes, volume, groups), out_shap...  23.4 us
    pallas_call x1, Pallas kernels, per_device(): pl.pallas_call(store_kernel, out_shape=(jax.ShapeDtypeStruct(block, f32),...  1.04 us

profile of v6, /device:TPU:0, one launch (start us, length us, event | category | flops | bytes accessed | tf_op | source)
XLA Modules:
  0.0 25.0 jit_solution(2164941832040217370)
XLA Ops:
  0.6 23.4 %md_step.1 = (f32[4,2,3,3,3,8,128]{6,5,4,3,2,1,0:T(8,128)S(1)}, f32[4,2,3,3,2,8,128]{6,5,4,3,2,1,0:T(8,128)S(1)}, f32[8,128]{1,0:T(8,128)S(1)}) custom-call(f32[4,2,3,3,2,8,128]{6,5,4,3,2,1,0:T(8,128)} %links_in.1, f32[4,2,3,3,2,8,128]{6,5,4,3,2,1,0:T(8,128)} %mom_in.1), custom_call_target="tpu_custom_call" | custom-call | tf_op jit(solution)/shard_map/md_step/pallas_call | solution.py:774
  24.0 1.0 %store.1 = (f32[4,2,3,3,2,8,128]{6,5,4,3,2,1,0:T(8,128)}, f32[4,2,3,3,2,8,128]{6,5,4,3,2,1,0:T(8,128)}, f32[1,128]{1,0:T(1,128)}) custom-call(f32[4,2,3,3,3,8,128]{6,5,4,3,2,1,0:T(8,128)S(1)} %get-tuple-element.9.links, f32[4,2,3,3,2,8,128]{6,5,4,3,2,1,0:T(8,128)S(1)} %get-tuple-element.10.mom, f32[8,128]{1,0:T(8,128)S(1)} %get-tuple-element.11.plaq), custom_call_target="tpu_custom_call" | custom-call | tf_op jit(solution)/shard_map/store/pallas_call | solution.py:825

commit v7 on v6

--- a/solution.py
+++ b/solution.py
@@ -14,12 +14,12 @@
     ((1, 3), (0, 3), (0, 1), (2, 3), (1, 2), (0, 2)),
     ((1, 3), (2, 3), (0, 3), (0, 2), (0, 1), (1, 2)),
 )
-EARLY = 2
+EARLY = 3
 EDGE = (3, 0, 2)
 LOADS = (3, 1, 0, 2)
 Z_LINKS = (3, 0, 1)
 SENDS = ((0, 3), (1, 3), (2, 3), (1, 0), (1, 2), (2, 1), (0, 1), (2, 0), (0, 2))
-UPDATES = (3, 0, 1, 2)
+UPDATES = (3, 2, 0, 1)
 MESH_ID = pl.DeviceIdType.MESH
 
 kick_size = 0.25

time: 25.2 us -> 24.9 us (0.988)
  Pallas kernels: 24.4 us -> 24.1 us
    pallas_call x1, Pallas kernels: 23.4 us -> 23.1 us  [per_device(): pl.pallas_call(functools.partial(kernel, sizes, volume, groups), out_shap...]
where the time goes in v7:
time: 24.9 us; the launch traced here: 24.7 us
  Pallas kernels  24.1 us (97%)
  between operations  0.64 us (3%)
    pallas_call x1, Pallas kernels, per_device(): pl.pallas_call(functools.partial(kernel, sizes, volume, groups), out_shap...  23.1 us
    pallas_call x1, Pallas kernels, per_device(): pl.pallas_call(store_kernel, out_shape=(jax.ShapeDtypeStruct(block, f32),...  1.04 us

profile of v7, /device:TPU:0, one launch (start us, length us, event | category | flops | bytes accessed | tf_op | source)
XLA Modules:
  0.0 24.7 jit_solution(16093423139721481499)
XLA Ops:
  0.6 23.1 %md_step.1 = (f32[4,2,3,3,3,8,128]{6,5,4,3,2,1,0:T(8,128)S(1)}, f32[4,2,3,3,2,8,128]{6,5,4,3,2,1,0:T(8,128)S(1)}, f32[8,128]{1,0:T(8,128)S(1)}) custom-call(f32[4,2,3,3,2,8,128]{6,5,4,3,2,1,0:T(8,128)} %links_in.1, f32[4,2,3,3,2,8,128]{6,5,4,3,2,1,0:T(8,128)} %mom_in.1), custom_call_target="tpu_custom_call" | custom-call | tf_op jit(solution)/shard_map/md_step/pallas_call | solution.py:774
  23.7 1.0 %store.1 = (f32[4,2,3,3,2,8,128]{6,5,4,3,2,1,0:T(8,128)}, f32[4,2,3,3,2,8,128]{6,5,4,3,2,1,0:T(8,128)}, f32[1,128]{1,0:T(1,128)}) custom-call(f32[4,2,3,3,3,8,128]{6,5,4,3,2,1,0:T(8,128)S(1)} %get-tuple-element.9.links, f32[4,2,3,3,2,8,128]{6,5,4,3,2,1,0:T(8,128)S(1)} %get-tuple-element.10.mom, f32[8,128]{1,0:T(8,128)S(1)} %get-tuple-element.11.plaq), custom_call_target="tpu_custom_call" | custom-call | tf_op jit(solution)/shard_map/store/pallas_call | solution.py:825

commit v8 on v7

--- a/solution.py
+++ b/solution.py
@@ -17,7 +17,7 @@
 EARLY = 3
 EDGE = (3, 0, 2)
 LOADS = (3, 1, 0, 2)
-Z_LINKS = (3, 0, 1)
+Z_LINKS = (3, 1, 0)
 SENDS = ((0, 3), (1, 3), (2, 3), (1, 0), (1, 2), (2, 1), (0, 1), (2, 0), (0, 2))
 UPDATES = (3, 2, 0, 1)
 MESH_ID = pl.DeviceIdType.MESH

time: 24.9 us -> 24.9 us (level)
  no operation moved by 1% of the time
where the time goes in v8:
time: 24.9 us; the launch traced here: 24.7 us
  Pallas kernels  24.1 us (97%)
  between operations  0.64 us (3%)
    pallas_call x1, Pallas kernels, per_device(): pl.pallas_call(functools.partial(kernel, sizes, volume, groups), out_shap...  23.1 us
    pallas_call x1, Pallas kernels, per_device(): pl.pallas_call(store_kernel, out_shape=(jax.ShapeDtypeStruct(block, f32),...  1.04 us

profile of v8, /device:TPU:0, one launch (start us, length us, event | category | flops | bytes accessed | tf_op | source)
XLA Modules:
  0.0 24.7 jit_solution(1252397778675734756)
XLA Ops:
  0.6 23.1 %md_step.1 = (f32[4,2,3,3,3,8,128]{6,5,4,3,2,1,0:T(8,128)S(1)}, f32[4,2,3,3,2,8,128]{6,5,4,3,2,1,0:T(8,128)S(1)}, f32[8,128]{1,0:T(8,128)S(1)}) custom-call(f32[4,2,3,3,2,8,128]{6,5,4,3,2,1,0:T(8,128)} %links_in.1, f32[4,2,3,3,2,8,128]{6,5,4,3,2,1,0:T(8,128)} %mom_in.1), custom_call_target="tpu_custom_call" | custom-call | tf_op jit(solution)/shard_map/md_step/pallas_call | solution.py:774
  23.7 1.0 %store.1 = (f32[4,2,3,3,2,8,128]{6,5,4,3,2,1,0:T(8,128)}, f32[4,2,3,3,2,8,128]{6,5,4,3,2,1,0:T(8,128)}, f32[1,128]{1,0:T(1,128)}) custom-call(f32[4,2,3,3,3,8,128]{6,5,4,3,2,1,0:T(8,128)S(1)} %get-tuple-element.9.links, f32[4,2,3,3,2,8,128]{6,5,4,3,2,1,0:T(8,128)S(1)} %get-tuple-element.10.mom, f32[8,128]{1,0:T(8,128)S(1)} %get-tuple-element.11.plaq), custom_call_target="tpu_custom_call" | custom-call | tf_op jit(solution)/shard_map/store/pallas_call | solution.py:825
